TPU v7x, 32 devices: a whole 2x2x4 slice. The times are simulated.
32 devices in a mesh: row: 4 (over y, x), col: 8 (over z, core).
Axes of the slice: x: 2, y: 2, z: 4, core: 2. Of those that a mesh axis runs over, the one named last changes fastest.
Arguments:
- out_grad: bfloat16 [4096, 512], P('col', 'row'), may hold values from -6 to 6
- node_in: bfloat16 [4096, 512], P(('row', 'col')), may hold values from -0.09375 to 0.09375
- weights: bfloat16 [3, 512, 512], replicated, may hold values from -0.25 to 0.25
- tile_vals: bfloat16 [3, 8, 4, 32, 128, 128], P(None, 'col', 'row'), may hold values from -0.15625 to 0.15625
- tile_rows: int32 [3, 8, 4, 32], P(None, 'col', 'row'), may hold values from 0 to 3
- tile_cols: int32 [3, 8, 4, 32], P(None, 'col', 'row'), may hold values from 0 to 7
- tile_count: int32 [3, 8, 4], P(None, 'col', 'row'), may hold values from 1 to 32, as said below
Outputs:
- d_nodes: bfloat16 [4096, 512], P(('row', 'col'))
- d_weights: float32 [3, 512, 512], replicated
Inputs may be any that keep to these rules, and one draw needn't show every extreme that they name: Only the first tile_count slots of a block's list hold tiles; later slots are ignored. In every relation some block uses all 32 slots. `tile_rows`: coordinates may repeat within a block's list; such tiles add.
All inputs are finite; a program needn't handle non-finite values.
Results may differ from a plain program's by a relative error of at most 0.005.
Values may be sent and summed in bfloat16 or wider, within the bound.
A program may use at most 256 MiB of HBM per device.

v0:
```python
import functools

import jax
import jax.numpy as jnp
from jax import lax
from jax.experimental import pallas as pl
from jax.experimental.pallas import tpu as pltpu
from jax.sharding import PartitionSpec as P

MESH = pl.DeviceIdType.MESH
F32 = jnp.float32
BF16 = jnp.bfloat16


def assemble_kernel(rows_ref, cols_ref, count_ref, tiles_ref, out_ref, total):
    relation = pl.program_id(0)
    tile_rows, tile_cols, tile = total.shape[0], total.shape[1], total.shape[2]
    for i in range(tile_rows):
        for j in range(tile_cols):
            total[i, j] = jnp.zeros((tile, tile), F32)

    def add_tile(slot, carry):
        i = rows_ref[relation, 0, 0, slot]
        j = cols_ref[relation, 0, 0, slot]
        total[i, j] = total[i, j] + tiles_ref[0, slot].astype(F32)
        return carry

    lax.fori_loop(0, count_ref[relation], add_tile, 0)
    for i in range(tile_rows):
        for j in range(tile_cols):
            out_ref[i * tile : (i + 1) * tile, j * tile : (j + 1) * tile] = total[i, j].astype(BF16)


def assemble(tile_vals, tile_rows, tile_cols, tile_count, targets, sources):
    relations, cap, tile = tile_vals.shape[0], tile_vals.shape[3], tile_vals.shape[4]
    vals = tile_vals.reshape(relations, cap, tile, tile)
    return pl.pallas_call(
        assemble_kernel,
        grid_spec=pltpu.PrefetchScalarGridSpec(
            num_scalar_prefetch=3,
            grid=(relations,),
            in_specs=[pl.BlockSpec((1, cap, tile, tile), lambda r, *_: (r, 0, 0, 0))],
            out_specs=pl.BlockSpec((targets, sources), lambda r, *_: (r, 0)),
            scratch_shapes=[pltpu.VMEM((targets // tile, sources // tile, tile, tile), F32)],
        ),
        out_shape=jax.ShapeDtypeStruct((relations * targets, sources), BF16),
        compiler_params=pltpu.CompilerParams(vmem_limit_bytes=60 * 2**20),
    )(
        tile_rows,
        tile_cols,
        tile_count.reshape(relations),
        vals,
    )


def main_kernel(
    nr, nc, relations,
    grad_ref, nodes_ref, w_hbm, a_hbm,
    dn_ref, ag_ref,
    gslot, g, w, a, xall, pt, nsend, nrecv, ncomb, ndst,
    dw, dwrecv, pbuf, precv, zbuf, zrecv,
    load_sem, gs, gr, xs, xr, fs, fr, ns, nrs, nzs, nzr, ds, dr, ps, pr, zs, zr,
    azs, azr, aps, apr, acs, acr,
):
    nz = nc // 2
    tn = grad_ref.shape[0]
    width = grad_ref.shape[1]
    nd = nodes_ref.shape[0]
    f = w_hbm.shape[1]
    me_r = lax.axis_index("row")
    me_c = lax.axis_index("col")
    z = me_c // 2
    core = me_c % 2
    other = 1 - core
    sibling = {"col": z * 2 + other}

    def row_peer(d):
        return {"row": lax.rem(me_r + d, nr)}

    def z_peer(d):
        return {"col": lax.rem(z + d, nz) * 2 + core}

    def remote(src, dst, send, recv, dev):
        return pltpu.make_async_remote_copy(
            src_ref=src, dst_ref=dst, send_sem=send, recv_sem=recv, device_id=dev, device_id_type=MESH
        )

    def x_slot(k):
        return xall.at[pl.ds(pl.multiple_of(k * nd, nd), nd), :]

    load_a = pltpu.make_async_copy(a_hbm, a, load_sem.at[0])
    load_w = pltpu.make_async_copy(w_hbm, w, load_sem.at[1])
    load_w.start()
    load_a.start()

    barrier = pltpu.get_barrier_semaphore()
    for d in range(1, nr):
        pl.semaphore_signal(barrier, inc=1, device_id=row_peer(d), device_id_type=MESH)
    for d in range(1, nz):
        pl.semaphore_signal(barrier, inc=1, device_id=z_peer(d), device_id_type=MESH)
    pl.semaphore_signal(barrier, inc=1, device_id=sibling, device_id_type=MESH)
    pl.semaphore_wait(barrier, nr - 1 + nz - 1 + 1)

    g_copies = [
        remote(grad_ref, gslot.at[me_r], gs.at[d - 1], gr.at[d - 1], row_peer(d)) for d in range(1, nr)
    ]
    for c in g_copies:
        c.start()
    x_copies = [
        remote(nodes_ref, x_slot(me_c), xs.at[d - 1], xr.at[d - 1], z_peer(d)) for d in range(1, nz)
    ]
    for c in x_copies:
        c.start()
    f_copies = [remote(nodes_ref, x_slot(me_c), fs.at[0], fr.at[0], sibling)]
    f_copies[0].start()
    xall[pl.ds(pl.multiple_of(me_c * nd, nd), nd), :] = nodes_ref[...]
    gslot[me_r] = grad_ref[...]

    load_w.wait()
    for c in g_copies:
        c.wait_recv()
    for k in range(nr):
        g[:, k * width : (k + 1) * width] = gslot[k]
    for r in range(relations):
        pt[:, r * tn : (r + 1) * tn] = lax.dot_general(
            w[r], g[...], (((1,), (1,)), ((), ())), preferred_element_type=F32
        ).astype(BF16)
    load_a.wait()

    def mix(k, carry):
        cols = pl.ds(pl.multiple_of(k * 2 * nd, 2 * nd), 2 * nd)
        both = jnp.dot(pt[...], a[:, cols], preferred_element_type=F32)
        nsend[0, k] = both[:, :nd]
        nsend[1, k] = both[:, nd:]
        return carry

    lax.fori_loop(0, nz, mix, 0)
    n_core = remote(nsend.at[other], nrecv, ns.at[0], nrs.at[0], sibling)
    n_core.start()

    for d in range(1, nz):
        x_copies[d - 1].wait_recv()
        slot = lax.rem(z + nz - d, nz) * 2 + core
        c = remote(x_slot(slot), x_slot(slot), fs.at[d], fr.at[d], sibling)
        c.start()
        f_copies.append(c)

    n_core.wait_recv()

    def combine(k, carry):
        ncomb[k] = (nsend[core, k] + nrecv[k]).astype(BF16)
        return carry

    lax.fori_loop(0, nz, combine, 0)
    n_copies = [
        remote(ncomb.at[lax.rem(z + d, nz)], ndst.at[d - 1], nzs.at[d - 1], nzr.at[d - 1], z_peer(d))
        for d in range(1, nz)
    ]
    for c in n_copies[:-1]:
        c.start()

    for c in f_copies:
        c.wait_recv()

    chunk = f // 2
    plane_rows = pbuf.shape[2]
    piece = zbuf.shape[2]
    sent = [[] for _ in range(relations)]
    batches = [[None] * relations for _ in range(5)]

    def launch(stage, r, copies):
        for c in copies:
            c.start()
        batches[stage][r] = copies
        sent[r].extend(copies)

    def arrived(stage, r):
        for c in batches[stage][r]:
            c.wait_recv()

    def terms(r):
        for h in range(2):
            y = jnp.dot(
                a[r * tn : (r + 1) * tn, :],
                xall[:, h * chunk : (h + 1) * chunk],
                preferred_element_type=F32,
            )
            dw[r, h] = jnp.dot(y.astype(BF16).T, g[...], preferred_element_type=F32)
        launch(0, r, [remote(dw.at[r, other], dwrecv.at[r], ds.at[r, 0], dr.at[r, 0], sibling)])

    def plane_scatter(r):
        arrived(0, r)
        for k in range(nr):
            rows = slice(k * plane_rows, (k + 1) * plane_rows)
            pbuf[r, k] = (dw[r, core, rows, :] + dwrecv[r, rows, :]).astype(BF16)
        launch(1, r, [
            remote(
                pbuf.at[r, lax.rem(me_r + d, nr)], precv.at[r, d - 1],
                ps.at[r, d - 1], pr.at[r, d - 1], row_peer(d),
            )
            for d in range(1, nr)
        ])

    def z_scatter(r):
        arrived(1, r)
        for k in range(nz):
            rows = slice(k * piece, (k + 1) * piece)
            part = pbuf[r, me_r, rows, :].astype(F32)
            for d in range(1, nr):
                part = part + precv[r, d - 1, rows, :].astype(F32)
            zbuf[r, k] = part.astype(BF16)
        launch(2, r, [
            remote(
                zbuf.at[r, lax.rem(z + d, nz)], zrecv.at[r, d - 1],
                zs.at[r, d - 1], zr.at[r, d - 1], z_peer(d),
            )
            for d in range(1, nz)
        ])

    def z_gather(r):
        arrived(2, r)
        final = zbuf[r, z].astype(F32)
        for d in range(1, nz):
            final = final + zrecv[r, d - 1].astype(F32)
        ag_ref[r, core, me_r, z] = final.astype(BF16)
        mine = ag_ref.at[r, core, me_r, z]
        launch(3, r, [remote(mine, mine, azs.at[r, d - 1], azr.at[r, d - 1], z_peer(d)) for d in range(1, nz)])

    last = [[] for _ in range(relations)]

    def plane_gather(r):
        arrived(3, r)
        mine = ag_ref.at[r, core, me_r]
        launch(4, r, [remote(mine, mine, aps.at[r, d - 1], apr.at[r, d - 1], row_peer(d)) for d in range(1, nr)])
        c = remote(mine, mine, acs.at[r, 0], acr.at[r, 0], sibling)
        c.start()
        last[r].append(c)

    def core_gather(r):
        for d in range(1, nr):
            batches[4][r][d - 1].wait_recv()
            slot = ag_ref.at[r, core, lax.rem(me_r + nr - d, nr)]
            c = remote(slot, slot, acs.at[r, d], acr.at[r, d], sibling)
            c.start()
            last[r].append(c)

    terms(0)
    for r in range(1, relations):
        terms(r)
        plane_scatter(r - 1)
    plane_scatter(relations - 1)
    stages = (z_scatter, z_gather, plane_gather, core_gather)
    for t in range(relations + len(stages) - 1):
        for stage in range(len(stages)):
            if 0 <= t - stage < relations:
                stages[stage](t - stage)
        if t == relations:
            n_copies[-1].start()

    for c in n_copies:
        c.wait_recv()
    own = nsend[core, z] + nrecv[z]
    for d in range(1, nz):
        own = own + ndst[d - 1].astype(F32)
    dn_ref[...] = own.T.astype(BF16)

    for r in range(relations):
        for c in last[r]:
            c.wait_recv()
        for c in sent[r] + last[r]:
            c.wait_send()
    for c in g_copies + x_copies + f_copies + [n_core] + n_copies:
        c.wait_send()


def widen_kernel(dn_ref, dw_ref, dn_out, dw_out, nodes, narrow, wide, in_sem, out_sem):
    parts, rows = narrow.shape[0], narrow.shape[1]

    def part(ref, k):
        return ref.at[k * rows : (k + 1) * rows, :]

    loads = [pltpu.make_async_copy(part(dw_ref, k), narrow.at[k], in_sem.at[k]) for k in range(parts)]
    stores = [pltpu.make_async_copy(wide.at[k], part(dw_out, k), out_sem.at[k]) for k in range(parts)]
    loads.append(pltpu.make_async_copy(dn_ref, nodes, in_sem.at[parts]))
    stores.append(pltpu.make_async_copy(nodes, dn_out, out_sem.at[parts]))
    for c in loads:
        c.start()
    for k in range(parts):
        loads[k].wait()
        wide[k] = narrow[k].astype(F32)
        stores[k].start()
    loads[parts].wait()
    stores[parts].start()
    for c in stores:
        c.wait()


def widen(d_nodes, gathered):
    total, f = gathered.shape
    parts = 6 if total % 96 == 0 else 1
    rows = total // parts
    hbm = pl.BlockSpec(memory_space=pltpu.HBM)
    return pl.pallas_call(
        widen_kernel,
        in_specs=[hbm, hbm],
        out_specs=(hbm, hbm),
        out_shape=(
            jax.ShapeDtypeStruct(d_nodes.shape, BF16),
            jax.ShapeDtypeStruct(gathered.shape, F32),
        ),
        scratch_shapes=[
            pltpu.VMEM(d_nodes.shape, BF16),
            pltpu.VMEM((parts, rows, f), BF16),
            pltpu.VMEM((parts, rows, f), F32),
            pltpu.SemaphoreType.DMA((parts + 1,)),
            pltpu.SemaphoreType.DMA((parts + 1,)),
        ],
    )(d_nodes, gathered)


def body(nr, nc, out_grad, node_in, weights, tile_vals, tile_rows, tile_cols, tile_count):
    relations, f = weights.shape[0], weights.shape[1]
    tn, width = out_grad.shape
    nd = node_in.shape[0]
    sn = nd * nc
    nz = nc // 2
    half = f // 2
    plane_rows = half // nr
    piece = plane_rows // nz
    dense = assemble(tile_vals, tile_rows, tile_cols, tile_count, tn, sn)
    dma = lambda *n: pltpu.SemaphoreType.DMA(n)
    vmem = pl.BlockSpec(memory_space=pltpu.VMEM)
    hbm = pl.BlockSpec(memory_space=pltpu.HBM)
    d_nodes, gathered = pl.pallas_call(
        functools.partial(main_kernel, nr, nc, relations),
        out_shape=(
            jax.ShapeDtypeStruct((nd, f), BF16),
            jax.ShapeDtypeStruct((relations, 2, nr, nz, piece, f), BF16),
        ),
        in_specs=[vmem, vmem, hbm, hbm],
        out_specs=(vmem, vmem),
        scratch_shapes=[
            pltpu.VMEM((nr, tn, width), BF16),
            pltpu.VMEM((tn, f), BF16),
            pltpu.VMEM(weights.shape, BF16),
            pltpu.VMEM((relations * tn, sn), BF16),
            pltpu.VMEM((sn, f), BF16),
            pltpu.VMEM((f, relations * tn), BF16),
            pltpu.VMEM((2, nz, f, nd), F32),
            pltpu.VMEM((nz, f, nd), F32),
            pltpu.VMEM((nz, f, nd), BF16),
            pltpu.VMEM((nz - 1, f, nd), BF16),
            pltpu.VMEM((relations, 2, half, f), F32),
            pltpu.VMEM((relations, half, f), F32),
            pltpu.VMEM((relations, nr, plane_rows, f), BF16),
            pltpu.VMEM((relations, nr - 1, plane_rows, f), BF16),
            pltpu.VMEM((relations, nz, piece, f), BF16),
            pltpu.VMEM((relations, nz - 1, piece, f), BF16),
            dma(2),
            dma(nr - 1), dma(nr - 1),
            dma(nz - 1), dma(nz - 1),
            dma(nz), dma(nz),
            dma(1), dma(1),
            dma(nz - 1), dma(nz - 1),
            dma(relations, 1), dma(relations, 1),
            dma(relations, nr - 1), dma(relations, nr - 1),
            dma(relations, nz - 1), dma(relations, nz - 1),
            dma(relations, nz - 1), dma(relations, nz - 1),
            dma(relations, nr - 1), dma(relations, nr - 1),
            dma(relations, nr), dma(relations, nr),
        ],
        compiler_params=pltpu.CompilerParams(
            collective_id=0, has_side_effects=True, vmem_limit_bytes=67043328
        ),
    )(out_grad, node_in, weights, dense)
    d_nodes, d_weights = widen(d_nodes, gathered.reshape(relations * f, f))
    return d_nodes, d_weights.reshape(relations, f, f)


def solution(mesh):
    return jax.shard_map(
        functools.partial(body, mesh.shape["row"], mesh.shape["col"]),
        mesh=mesh,
        in_specs=(
            P("col", "row"),
            P(("row", "col"), None),
            P(),
            P(None, "col", "row", None, None, None),
            P(None, "col", "row", None),
            P(None, "col", "row", None),
            P(None, "col", "row"),
        ),
        out_specs=(P(("row", "col"), None), P()),
        check_vma=False,
    )
```

profile of v0, /device:TPU:0, one launch (start us, length us, event | category | flops | bytes accessed | tf_op | source)
XLA Modules:
  0.0 60.3 jit_solution(5539360638715369462)
XLA Ops:
  0.6 5.6 %shard_map.86.a_hbm = bf16[1536,1024]{1,0:T(8,128)(2,1)} custom-call(s32[3,1,1,32]{3,2,1,0:T(1,128)} %rows_ref.1, s32[3,1,1,32]{3,2,1,0:T(1,128)} %cols_ref.1, s32[3]{0:T(128)} %bitcast.6, bf16[3,32,128,128]{3,2,1,0:T(8,128)(2,1)} %bitcast.4), custom_call_target="tpu_custom_call" | custom-call | tf_op jit(solution)/shard_map/pallas_call | solution.py:37
  6.2 51.3 %shard_map.87 = (bf16[128,512]{1,0:T(8,128)(2,1)}, bf16[3,2,4,4,16,512]{5,4,3,2,1,0:T(8,128)(2,1)}) custom-call(bf16[512,128]{1,0:T(8,128)(2,1)} %grad_ref.1, bf16[128,512]{1,0:T(8,128)(2,1)} %nodes_ref.1, bf16[3,512,512]{2,1,0:T(8,128)(2,1)} %w_hbm.1, bf16[1536,1024]{1,0:T(8,128)(2,1)} %shard_map.86.a_hbm), custom_call_target="tpu_custom_call" | custom-call | tf_op jit(solution)/shard_map/pallas_call | solution.py:334
  57.5 2.8 %shard_map.88 = (bf16[128,512]{1,0:T(8,128)(2,1)}, f32[1536,512]{1,0:T(8,128)}) custom-call(bf16[128,512]{1,0:T(8,128)(2,1)} %get-tuple-element.6.dn_ref, bf16[1536,512]{1,0:T(8,128)(2,1)} %bitcast.5), custom_call_target="tpu_custom_call" | custom-call | tf_op jit(solution)/shard_map/pallas_call | solution.py:303
where the time goes:
time: 60.5 us; the launch traced here: 60.3 us
  Pallas kernels  59.7 us (99%)
  between operations  0.64 us (1%)
    pallas_call x1, Pallas kernels, body(): pl.pallas_call(functools.partial(main_kernel, nr, nc, relations), out_sha...  51.3 us
    pallas_call x1, Pallas kernels, assemble(): pl.pallas_call(assemble_kernel, grid_spec=pltpu.PrefetchScalarGridSpec(nu...  5.6 us
    pallas_call x1, Pallas kernels, widen(): pl.pallas_call(widen_kernel, in_specs=[hbm, hbm], out_specs=(hbm, hbm), o...  2.8 us

commit v1 on v0

v1 whole, which is shorter than its diff:
```python
import functools

import jax
import jax.numpy as jnp
from jax import lax
from jax.experimental import pallas as pl
from jax.experimental.pallas import tpu as pltpu
from jax.sharding import PartitionSpec as P

MESH = pl.DeviceIdType.MESH
F32 = jnp.float32
BF16 = jnp.bfloat16
I32 = jnp.int32
HALVES = 2
scope = jax.named_scope


def reduce_order(chunks):
    link, hop = 1.4, 3.3
    events = []
    for k in range(chunks):
        t = link * k
        for stage, at in ((2, t), (3, t + hop), (4, t + 2 * hop), (5, t + 3 * hop)):
            events.append((at, stage, k))
    return [(stage, k) for _, stage, k in sorted(events)]


def main_kernel(
    nr, nc, relations, tile_cols_n,
    rows_hbm, cols_hbm, count_hbm, vals_hbm, grad_hbm, nodes_hbm, w_hbm,
    dn_ref, ag_ref,
    rows_v, cols_v, count_v, table_v, table_s, vals, chain, gslot, g, w, a, xall, pt,
    nsend, nrecv, ndst, nfin, pbuf, crecv, precv, zbuf, zrecv,
    small_sem, val_sem, load_sem, gs, gr, xs, xr, fs, fr, ns, nrs, nzs, nzr, nfs, nfr,
    cs, cr, ps, pr, zs, zr, azs, azr, aps, apr, acs, acr,
):
    nz = nc // 2
    cap, tile = vals.shape[1], vals.shape[2]
    tn, width = gslot.shape[1], gslot.shape[2]
    nd = nodes_hbm.shape[0]
    f = w_hbm.shape[1]
    tile_rows_n = tn // tile
    half = f // HALVES
    plane_rows = pbuf.shape[3]
    piece = zbuf.shape[2]
    lanes_f = f // tile
    chunks = relations * HALVES
    me_r = lax.axis_index("row")
    me_c = lax.axis_index("col")
    z = me_c // 2
    core = me_c % 2
    sibling = {"col": z * 2 + 1 - core}
    lead = core == 1
    other = core == 0

    def row_peer(d):
        return {"row": lax.rem(me_r + d, nr)}

    def z_peer(d):
        return {"col": lax.rem(z + d, nz) * 2 + core}

    def remote(src, dst, send, recv, dev):
        return pltpu.make_async_remote_copy(
            src_ref=src, dst_ref=dst, send_sem=send, recv_sem=recv, device_id=dev, device_id_type=MESH
        )

    def x_slot(k):
        return xall.at[pl.ds(pl.multiple_of(k * nd, nd), nd), :]

    with scope("entry"):
        barrier = pltpu.get_barrier_semaphore()
        for d in range(1, nr):
            pl.semaphore_signal(barrier, inc=1, device_id=row_peer(d), device_id_type=MESH)
        for d in range(1, nz):
            pl.semaphore_signal(barrier, inc=1, device_id=z_peer(d), device_id_type=MESH)
        pl.semaphore_signal(barrier, inc=1, device_id=sibling, device_id_type=MESH)

        small = [
            pltpu.make_async_copy(rows_hbm, rows_v, small_sem.at[0]),
            pltpu.make_async_copy(cols_hbm, cols_v, small_sem.at[1]),
            pltpu.make_async_copy(count_hbm, count_v, small_sem.at[2]),
        ]
        load_g = pltpu.make_async_copy(grad_hbm, gslot.at[me_r], load_sem.at[0])
        load_x = pltpu.make_async_copy(nodes_hbm, x_slot(me_c), load_sem.at[1])
        load_w = pltpu.make_async_copy(w_hbm, w, load_sem.at[2])
        load_vals = [pltpu.make_async_copy(vals_hbm.at[r], vals.at[r], val_sem.at[r]) for r in range(relations)]
        load_g.start()
        load_x.start()
        for c in small:
            c.start()
        for c in load_vals:
            c.start()
        load_w.start()

    with scope("tables"):
        for c in small:
            c.wait()
        spread = table_v.shape[1]
        slot_lane = lax.broadcasted_iota(I32, (1, cap), 1)
        slot_row = lax.broadcasted_iota(I32, (cap, cap), 0)
        slot_col = lax.broadcasted_iota(I32, (cap, cap), 1)
        place_row = lax.broadcasted_iota(I32, (cap, spread), 0)
        place_col = lax.broadcasted_iota(I32, (cap, spread), 1)
        for r in range(relations):
            key = rows_v[r, 0] * tile_cols_n + cols_v[r, 0]
            key = jnp.where(slot_lane < count_v[0:1, r : r + 1], key, -1)
            down = jnp.max(jnp.where(slot_row == slot_col, jnp.broadcast_to(key, (cap, cap)), -1), axis=1, keepdims=True)
            same = (down == key) & (slot_row < slot_col)
            before = jnp.max(jnp.where(same, slot_row + 1, 0), axis=0, keepdims=True)
            last = jnp.max(jnp.where(down == place_col, place_row + 1, 0), axis=0, keepdims=True)
            table_v[r : r + 1, 0:cap] = before
            table_v[relations + r : relations + r + 1, :] = last
        load_table = pltpu.make_async_copy(table_v, table_s, small_sem.at[3])
        load_table.start()

    with scope("barrier"):
        pl.semaphore_wait(barrier, nr - 1 + nz - 1 + 1)
        load_g.wait()
    with scope("sends"):
        mine = gslot.at[me_r]
        g_copies = [remote(mine, mine, gs.at[d - 1], gr.at[d - 1], row_peer(d)) for d in range(1, nr)]
        for c in g_copies:
            c.start()
        load_x.wait()
        own_x = x_slot(me_c)
        x_copies = [remote(own_x, own_x, xs.at[d - 1], xr.at[d - 1], z_peer(d)) for d in range(1, nz)]
        for c in x_copies:
            c.start()
        f_copies = [remote(own_x, own_x, fs.at[0], fr.at[0], sibling)]
        f_copies[0].start()

    with scope("chain"):
        load_table.wait()
        for c in load_vals:
            c.wait()
        for r in range(relations):
            chain[r, 0] = jnp.zeros((tile, tile), F32)

        def link(s, carry):
            for r in range(relations):
                chain[r, s + 1] = chain[r, table_s[r, s]] + vals[r, s].astype(F32)
            return carry

        lax.fori_loop(0, cap, link, 0)

    with scope("place"):

        def place(i, carry):
            def one(j, inner):
                for r in range(relations):
                    rows = pl.ds(pl.multiple_of(r * tn + i * tile, tile), tile)
                    cols = pl.ds(pl.multiple_of(j * tile, tile), tile)
                    a[rows, cols] = chain[r, table_s[relations + r, i * tile_cols_n + j]].astype(BF16)
                return inner

            return lax.fori_loop(0, tile_cols_n, one, carry)

        lax.fori_loop(0, tile_rows_n, place, 0)

    def forward(d):
        x_copies[d - 1].wait_recv()
        slot = x_slot(lax.rem(z + nz - d, nz) * 2 + core)
        c = remote(slot, slot, fs.at[d], fr.at[d], sibling)
        c.start()
        f_copies.append(c)

    def y_block(d):
        both = pl.ds(pl.multiple_of(lax.rem(z + nz - d, nz) * 2 * nd, 2 * nd), 2 * nd)
        for r in range(relations):
            part = jnp.dot(a[r * tn : (r + 1) * tn, both], xall[both, :], preferred_element_type=F32)
            for i in range(tile_rows_n):
                for j in range(lanes_f):
                    b = part[i * tile : (i + 1) * tile, j * tile : (j + 1) * tile]
                    at = i * lanes_f + j
                    if d > 0:
                        b = b + chain[r, at]
                    if d < nz - 1:
                        chain[r, at] = b
                    else:
                        pt[j * tile : (j + 1) * tile, r * tn + i * tile : r * tn + (i + 1) * tile] = b.astype(BF16).T

    with scope("y0"):
        f_copies[0].wait_recv()
        y_block(0)
    with scope("fwd1"):
        if nz > 1:
            forward(1)
    with scope("waitg"):
        load_w.wait()
        for c in g_copies:
            c.wait_recv()
    with scope("premix"):
        for k in range(nr):
            g[:, k * width : (k + 1) * width] = gslot[k]
        for r in range(relations):
            pt[:, r * tn : (r + 1) * tn] = lax.dot_general(
                w[r], g[...], (((1,), (1,)), ((), ())), preferred_element_type=F32
            ).astype(BF16)
    with scope("fwd2"):
        if nz > 2:
            forward(2)

    def mix(k, carry):
        cols = pl.ds(pl.multiple_of(k * 2 * nd, 2 * nd), 2 * nd)
        both = jnp.dot(pt[...], a[:, cols], preferred_element_type=F32)
        nsend[k, 0] = both[:, :nd].astype(BF16)
        nsend[k, 1] = both[:, nd:].astype(BF16)
        return carry

    with scope("mix"):
        lax.fori_loop(0, nz, mix, 0)

        @pl.when(lead)
        def _():
            remote(nsend, nrecv, ns.at[0], nrs.at[0], sibling).start()

    with scope("fwd3"):
        for d in range(3, nz):
            forward(d)

    for d in range(1, nz):
        with scope(f"y{d}"):
            f_copies[d].wait_recv()
            y_block(d)

    def n_core():
        return remote(nsend, nrecv, ns.at[0], nrs.at[0], sibling)

    def own_dn():
        return remote(nfin, dn_ref, nfs.at[0], nfr.at[0], sibling)

    def dn_copies():
        return [
            remote(nsend.at[lax.rem(z + d, nz)], ndst.at[d - 1], nzs.at[d - 1], nzr.at[d - 1], z_peer(d))
            for d in range(1, nz)
        ]

    def c_copy(k):
        r, h = k // HALVES, k % HALVES
        return remote(pbuf.at[r, h], crecv.at[r, h], cs.at[k], cr.at[k], sibling)

    def p_copies(k):
        r, h = k // HALVES, k % HALVES
        return [
            remote(
                pbuf.at[r, h, lax.rem(me_r + d, nr)], precv.at[k, d - 1],
                ps.at[k, d - 1], pr.at[k, d - 1], row_peer(d),
            )
            for d in range(1, nr)
        ]

    def z_copies(k):
        return [
            remote(
                zbuf.at[k, lax.rem(z + d, nz)], zrecv.at[k, d - 1],
                zs.at[k, d - 1], zr.at[k, d - 1], z_peer(d),
            )
            for d in range(1, nz)
        ]

    def za_copies(k):
        part = ag_ref.at[k // HALVES, k % HALVES, me_r, z]
        return [remote(part, part, azs.at[k, d - 1], azr.at[k, d - 1], z_peer(d)) for d in range(1, nz)]

    def pa_copies(k):
        part = ag_ref.at[k // HALVES, k % HALVES, me_r]
        return [remote(part, part, aps.at[k, d - 1], apr.at[k, d - 1], row_peer(d)) for d in range(1, nr)]

    def ca_copy(k, d):
        part = ag_ref.at[k // HALVES, k % HALVES, lax.rem(me_r + nr - d, nr)]
        return remote(part, part, acs.at[k, d], acr.at[k, d], sibling)

    def begin(copies):
        for c in copies:
            c.start()

    def arrived(copies):
        for c in copies:
            c.wait_recv()

    def left(copies):
        for c in copies:
            c.wait_send()

    def held_rows(r, h, q):
        first = h * half + q * plane_rows
        block, off = first // tile, first % tile
        assert off + plane_rows <= tile
        return jnp.concatenate(
            [chain[r, block * lanes_f + j, off : off + plane_rows, :] for j in range(lanes_f)], axis=1
        )

    def terms(k):
        r, h = k // HALVES, k % HALVES
        v = jnp.dot(pt[h * half : (h + 1) * half, r * tn : (r + 1) * tn], g[...], preferred_element_type=F32)
        for i in range(half // tile):
            for j in range(lanes_f):
                at = (h * (half // tile) + i) * lanes_f + j
                chain[r, at] = v[i * tile : (i + 1) * tile, j * tile : (j + 1) * tile]

        @pl.when(other)
        def _():
            for q in range(nr):
                pbuf[r, h, q] = held_rows(r, h, q).astype(BF16)
            c_copy(k).start()

    def plane_scatter(k):
        r, h = k // HALVES, k % HALVES
        c_copy(k).wait_recv()
        for q in range(nr):
            pbuf[r, h, q] = (held_rows(r, h, q) + crecv[r, h, q].astype(F32)).astype(BF16)
        begin(p_copies(k))

    def z_scatter(k):
        r, h = k // HALVES, k % HALVES
        arrived(p_copies(k))
        for q in range(nz):
            rows = slice(q * piece, (q + 1) * piece)
            part = pbuf[r, h, me_r, rows, :].astype(F32)
            for d in range(1, nr):
                part = part + precv[k, d - 1, rows, :].astype(F32)
            zbuf[k, q] = part.astype(BF16)
        begin(z_copies(k))

    def z_gather(k):
        arrived(z_copies(k))
        final = zbuf[k, z].astype(F32)
        for d in range(1, nz):
            final = final + zrecv[k, d - 1].astype(F32)
        ag_ref[k // HALVES, k % HALVES, me_r, z] = final.astype(BF16)
        begin(za_copies(k))

    def plane_gather(k):
        arrived(za_copies(k))
        begin(pa_copies(k))
        ca_copy(k, 0).start()

    def core_gather(k):
        copies = pa_copies(k)
        for d in range(1, nr):
            copies[d - 1].wait_recv()
            ca_copy(k, d).start()

    behind = 3
    for k in range(chunks):
        with scope(f"terms{k}"):
            terms(k)
        if k >= behind:
            with scope(f"s1_{k - behind}"):

                @pl.when(lead)
                def _():
                    plane_scatter(k - behind)

    @pl.when(lead)
    def _():
        for k in range(max(chunks - behind, 0), chunks):
            with scope(f"s1_{k}"):
                plane_scatter(k)
        stages = {2: z_scatter, 3: z_gather, 4: plane_gather, 5: core_gather}
        for stage, k in reduce_order(chunks):
            with scope(f"s{stage}_{k}"):
                stages[stage](k)
        with scope("end"):
            own_dn().wait_recv()
            n_core().wait_send()
            for k in range(chunks):
                left(p_copies(k) + z_copies(k) + za_copies(k) + pa_copies(k))
                left([ca_copy(k, d) for d in range(nr)])

    @pl.when(other)
    def _():
        with scope("dn_wait"):
            n_core().wait_recv()

        def combine(d, carry):
            k = lax.rem(z + d, nz)
            nsend[k] = (nsend[k].astype(F32) + nrecv[k].astype(F32)).astype(BF16)
            return carry

        with scope("dn_comb"):
            lax.fori_loop(1, nz, combine, 0)
            begin(dn_copies())
        with scope("dn_recv"):
            arrived(dn_copies())
        with scope("dn_fin"):
            for part in range(2):
                own = nsend[z, part].astype(F32) + nrecv[z, part].astype(F32)
                for d in range(1, nz):
                    own = own + ndst[d - 1, part].astype(F32)
                done = own.T.astype(BF16)
                if part == 0:
                    dn_ref[...] = done
                else:
                    nfin[...] = done
            own_dn().start()
        with scope("oend"):
            for k in range(chunks):
                arrived([ca_copy(k, d) for d in range(nr)])
            left([c_copy(k) for k in range(chunks)])
            left(dn_copies())
            own_dn().wait_send()

    left(g_copies + x_copies + f_copies)


def widen_kernel(dn_ref, dw_ref, dn_out, dw_out, wide, out_sem):
    parts, rows = wide.shape[0], wide.shape[1]
    stores = [
        pltpu.make_async_copy(wide.at[k], dw_out.at[k * rows : (k + 1) * rows, :], out_sem.at[k])
        for k in range(parts)
    ]
    stores.append(pltpu.make_async_copy(dn_ref, dn_out, out_sem.at[parts]))
    stores[parts].start()
    for k in range(parts):
        wide[k] = dw_ref[k * rows : (k + 1) * rows, :].astype(F32)
        stores[k].start()
    for c in stores:
        c.wait()


def widen(d_nodes, gathered):
    total, f = gathered.shape
    parts = 6 if total % 96 == 0 else 1
    rows = total // parts
    hbm = pl.BlockSpec(memory_space=pltpu.HBM)
    vmem = pl.BlockSpec(memory_space=pltpu.VMEM)
    return pl.pallas_call(
        widen_kernel,
        in_specs=[vmem, vmem],
        out_specs=(hbm, hbm),
        out_shape=(
            jax.ShapeDtypeStruct(d_nodes.shape, BF16),
            jax.ShapeDtypeStruct(gathered.shape, F32),
        ),
        scratch_shapes=[
            pltpu.VMEM((parts, rows, f), F32),
            pltpu.SemaphoreType.DMA((parts + 1,)),
        ],
    )(
        pltpu.with_memory_space_constraint(d_nodes, pltpu.VMEM),
        pltpu.with_memory_space_constraint(gathered, pltpu.VMEM),
    )


def body(nr, nc, out_grad, node_in, weights, tile_vals, tile_rows, tile_cols, tile_count):
    relations, f = weights.shape[0], weights.shape[1]
    cap, tile = tile_vals.shape[3], tile_vals.shape[4]
    tn, width = out_grad.shape
    nd = node_in.shape[0]
    sn = nd * nc
    nz = nc // 2
    half = f // HALVES
    plane_rows = half // nr
    piece = plane_rows // nz
    chunks = relations * HALVES
    places = (tn // tile) * (sn // tile)
    spread = -(-max(places, cap) // 128) * 128
    blocks = max(cap + 1, (tn // tile) * (f // tile), (f // tile) ** 2)
    dma = lambda *n: pltpu.SemaphoreType.DMA(n)
    hbm = pl.BlockSpec(memory_space=pltpu.HBM)
    vmem = pl.BlockSpec(memory_space=pltpu.VMEM)
    d_nodes, gathered = pl.pallas_call(
        functools.partial(main_kernel, nr, nc, relations, sn // tile),
        out_shape=(
            pltpu.VMEM((nd, f), BF16),
            pltpu.VMEM((relations, HALVES, nr, nz, piece, f), BF16),
        ),
        in_specs=[hbm] * 7,
        out_specs=(vmem, vmem),
        scratch_shapes=[
            pltpu.VMEM(tile_rows.shape, I32),
            pltpu.VMEM(tile_cols.shape, I32),
            pltpu.VMEM((1, relations), I32),
            pltpu.VMEM((-(-2 * relations // 8) * 8, spread), I32),
            pltpu.SMEM((-(-2 * relations // 8) * 8, spread), I32),
            pltpu.VMEM((relations, cap, tile, tile), BF16),
            pltpu.VMEM((relations, blocks, tile, tile), F32),
            pltpu.VMEM((nr, tn, width), BF16),
            pltpu.VMEM((tn, f), BF16),
            pltpu.VMEM(weights.shape, BF16),
            pltpu.VMEM((relations * tn, sn), BF16),
            pltpu.VMEM((sn, f), BF16),
            pltpu.VMEM((f, relations * tn), BF16),
            pltpu.VMEM((nz, 2, f, nd), BF16),
            pltpu.VMEM((nz, 2, f, nd), BF16),
            pltpu.VMEM((nz - 1, 2, f, nd), BF16),
            pltpu.VMEM((nd, f), BF16),
            pltpu.VMEM((relations, HALVES, nr, plane_rows, f), BF16),
            pltpu.VMEM((relations, HALVES, nr, plane_rows, f), BF16),
            pltpu.VMEM((chunks, nr - 1, plane_rows, f), BF16),
            pltpu.VMEM((chunks, nz, piece, f), BF16),
            pltpu.VMEM((chunks, nz - 1, piece, f), BF16),
            dma(4), dma(relations), dma(3),
            dma(nr - 1), dma(nr - 1),
            dma(nz - 1), dma(nz - 1),
            dma(nz), dma(nz),
            dma(1), dma(1),
            dma(nz - 1), dma(nz - 1),
            dma(1), dma(1),
            dma(chunks), dma(chunks),
            dma(chunks, nr - 1), dma(chunks, nr - 1),
            dma(chunks, nz - 1), dma(chunks, nz - 1),
            dma(chunks, nz - 1), dma(chunks, nz - 1),
            dma(chunks, nr - 1), dma(chunks, nr - 1),
            dma(chunks, nr), dma(chunks, nr),
        ],
        compiler_params=pltpu.CompilerParams(
            collective_id=0, has_side_effects=True, vmem_limit_bytes=63000 * 1024
        ),
    )(
        tile_rows,
        tile_cols,
        tile_count.reshape(1, relations),
        tile_vals.reshape(relations, cap, tile, tile),
        out_grad,
        node_in,
        weights,
    )
    d_nodes, d_weights = widen(d_nodes, gathered.reshape(relations * f, f))
    return d_nodes, d_weights.reshape(relations, f, f)


def solution(mesh):
    return jax.shard_map(
        functools.partial(body, mesh.shape["row"], mesh.shape["col"]),
        mesh=mesh,
        in_specs=(
            P("col", "row"),
            P(("row", "col"), None),
            P(),
            P(None, "col", "row", None, None, None),
            P(None, "col", "row", None),
            P(None, "col", "row", None),
            P(None, "col", "row"),
        ),
        out_specs=(P(("row", "col"), None), P()),
        check_vma=False,
    )
```

time: 60.5 us -> 55.8 us (0.922)
  Pallas kernels: 59.7 us -> 55 us
    pallas_call x3 -> x2, Pallas kernels: 59.7 us -> 55 us  [the longest x1 53.2 us: body(): pl.pallas_call(functools.partial(main_kernel, nr, nc, relations, sn // ti...]
where the time goes in v1:
time: 55.8 us; the launch traced here: 55.6 us
  Pallas kernels  55 us (99%)
  between operations  0.64 us (1%)
    pallas_call x1, Pallas kernels, body(): pl.pallas_call(functools.partial(main_kernel, nr, nc, relations, sn // ti...  53.2 us
    pallas_call x1, Pallas kernels, widen(): pl.pallas_call(widen_kernel, in_specs=[vmem, vmem], out_specs=(hbm, hbm),...  1.76 us

profile of v1, /device:TPU:0, one launch (start us, length us, event | category | flops | bytes accessed | tf_op | source)
XLA Modules:
  0.0 55.6 jit_solution(1871685636826210939)
XLA Ops:
  0.6 53.2 %shard_map.86 = (bf16[128,512]{1,0:T(8,128)(2,1)S(1)}, bf16[3,2,4,4,16,512]{5,4,3,2,1,0:T(8,128)(2,1)S(1)}) custom-call(s32[3,1,1,32]{3,2,1,0:T(1,128)} %rows_hbm.1, s32[3,1,1,32]{3,2,1,0:T(1,128)} %cols_hbm.1, s32[1,3]{1,0:T(1,128)} %bitcast.6, bf16[3,32,128,128]{3,2,1,0:T(8,128)(2,1)} %bitcast.5, bf16[512,128]{1,0:T(8,128)(2,1)} %grad_hbm.1, ...), custom_call_target="tpu_custom_call" | custom-call | tf_op jit(solution)/shard_map/pallas_call | solution.py:463
  53.9 1.8 %shard_map.87 = (bf16[128,512]{1,0:T(8,128)(2,1)}, f32[1536,512]{1,0:T(8,128)}) custom-call(bf16[128,512]{1,0:T(8,128)(2,1)S(1)} %get-tuple-element.6.dn_ref, bf16[1536,512]{1,0:T(8,128)(2,1)S(1)} %bitcast.4), custom_call_target="tpu_custom_call" | custom-call | tf_op jit(solution)/shard_map/pallas_call | solution.py:428

commit v2 on v1

v2 whole, which is shorter than its diff:
```python
import functools

import jax
import jax.numpy as jnp
from jax import lax
from jax.experimental import pallas as pl
from jax.experimental.pallas import tpu as pltpu
from jax.sharding import PartitionSpec as P

MESH = pl.DeviceIdType.MESH
F32 = jnp.float32
BF16 = jnp.bfloat16
I32 = jnp.int32
HALVES = 2
scope = jax.named_scope


def reduce_order(chunks, first, hops):
    link, hop, late = 1.4, 2.6, 1.1
    events = []
    for k in range(chunks):
        t = link * k + (late if k >= first else 0.0)
        if k >= first:
            events.append((1.0 + 0.1 * k, 1, k))
        events += [(t, 2, k), (t + hop, 3, k), (t + hops * hop, 4, k), (t + hops * hop + 3.6, 5, k)]
    return [(stage, k) for _, stage, k in sorted(events)]


def main_kernel(
    nr, nc, relations, tile_cols_n,
    rows_hbm, cols_hbm, count_hbm, vals_hbm, grad_hbm, nodes_hbm, w_hbm,
    dn_ref, ag_ref,
    rows_v, cols_v, count_v, table_v, table_s, chain, gslot, g, w, a, xall, pt,
    nsend, nrecv, ndst, nfin, pbuf, crecv, precv, zbuf, zrecv,
    small_sem, val_sem, load_sem, gs, gr, xs, xr, fs, fr, ns, nrs, nzs, nzr, nfs, nfr,
    cs, cr, ps, pr, zs, zr, zos, zor, aps, apr, acs, acr,
):
    nz = nc // 2
    cap, tile = rows_v.shape[3], chain.shape[2]
    tn, width = gslot.shape[1], gslot.shape[2]
    nd = nodes_hbm.shape[0]
    f = w_hbm.shape[1]
    half = f // HALVES
    tile_rows_n = tn // tile
    lanes_f, lanes_h = f // tile, half // tile
    held_at = tile_rows_n * lanes_h
    plane_rows = pbuf.shape[3]
    chunks = relations * HALVES
    me_r = lax.axis_index("row")
    me_c = lax.axis_index("col")
    z = me_c // 2
    core = me_c % 2
    sibling = {"col": z * 2 + 1 - core}
    lead = core == 1
    other = core == 0

    def row_peer(d):
        return {"row": lax.rem(me_r + d, nr)}

    def z_at(k):
        return {"col": k * 2 + core}

    def z_peer(d):
        return z_at(lax.rem(z + d, nz))

    left_side = z < nz // 2
    inward = jnp.where(left_side, z + 1, z - 1)
    outward = jnp.where(left_side, z - 1, z + 1)
    has_outer = (z > 0) & (z < nz - 1)
    inner = (z == nz // 2 - 1) | (z == nz // 2)
    last_hop = jnp.where(inner, 1, 0)
    passes = jnp.where(has_outer, 1, 0)

    def remote(src, dst, send, recv, dev):
        return pltpu.make_async_remote_copy(
            src_ref=src, dst_ref=dst, send_sem=send, recv_sem=recv, device_id=dev, device_id_type=MESH
        )

    def x_slot(h, k):
        return xall.at[h, pl.ds(pl.multiple_of(k * nd, nd), nd), :]

    def x_from(d):
        return lax.rem(z + nz - d, nz) * 2 + core

    def begin(copies):
        for c in copies:
            c.start()

    with scope("entry"):
        barrier = pltpu.get_barrier_semaphore()
        for d in range(1, nr):
            pl.semaphore_signal(barrier, inc=1, device_id=row_peer(d), device_id_type=MESH)
        for d in range(1, nz):
            pl.semaphore_signal(barrier, inc=1, device_id=z_peer(d), device_id_type=MESH)
        pl.semaphore_signal(barrier, inc=1, device_id=sibling, device_id_type=MESH)

        small = [
            pltpu.make_async_copy(rows_hbm, rows_v, small_sem.at[0]),
            pltpu.make_async_copy(cols_hbm, cols_v, small_sem.at[1]),
            pltpu.make_async_copy(count_hbm, count_v, small_sem.at[2]),
        ]
        load_g = pltpu.make_async_copy(grad_hbm, gslot.at[me_r], load_sem.at[0])
        load_x = [
            pltpu.make_async_copy(nodes_hbm.at[:, h * half : (h + 1) * half], x_slot(h, me_c), load_sem.at[2 + h])
            for h in range(HALVES)
        ]
        load_w = pltpu.make_async_copy(w_hbm, w, load_sem.at[1])
        load_vals = pltpu.make_async_copy(vals_hbm, nsend.at[0 : vals_hbm.shape[0]], val_sem.at[0])
        load_g.start()
        begin(load_x)
        begin(small)
        load_vals.start()
        load_w.start()

    with scope("tables"):
        for c in small:
            c.wait()
        spread = table_v.shape[1]
        slot_lane = lax.broadcasted_iota(I32, (1, cap), 1)
        slot_row = lax.broadcasted_iota(I32, (cap, cap), 0)
        slot_col = lax.broadcasted_iota(I32, (cap, cap), 1)
        place_row = lax.broadcasted_iota(I32, (cap, spread), 0)
        place_col = lax.broadcasted_iota(I32, (cap, spread), 1)
        for r in range(relations):
            key = rows_v[r, 0] * tile_cols_n + cols_v[r, 0]
            key = jnp.where(slot_lane < count_v[0:1, r : r + 1], key, -1)
            down = jnp.max(jnp.where(slot_row == slot_col, jnp.broadcast_to(key, (cap, cap)), -1), axis=1, keepdims=True)
            same = (down == key) & (slot_row < slot_col)
            before = jnp.max(jnp.where(same, slot_row + 1, 0), axis=0, keepdims=True)
            last = jnp.max(jnp.where(down == place_col, place_row + 1, 0), axis=0, keepdims=True)
            table_v[r : r + 1, 0:cap] = before
            table_v[relations + r : relations + r + 1, :] = last
        load_table = pltpu.make_async_copy(table_v, table_s, small_sem.at[3])
        load_table.start()

    with scope("barrier"):
        pl.semaphore_wait(barrier, nr - 1 + nz - 1 + 1)
        load_g.wait()
    with scope("sends"):
        mine = gslot.at[me_r]
        begin([remote(mine, mine, gs.at[0], gr.at[0], row_peer(d)) for d in range(1, nr)])
        for h in range(HALVES):
            load_x[h].wait()
            own = x_slot(h, me_c)
            begin([remote(own, own, xs.at[0], xr.at[h, d - 1], z_peer(d)) for d in range(1, nz)])
            remote(own, own, fs.at[0], fr.at[h, 0], sibling).start()

    with scope("chain"):
        load_table.wait()
        load_vals.wait()
        for r in range(relations):
            chain[r, 0] = jnp.zeros((tile, tile), F32)

        def link(s, carry):
            for r in range(relations):
                t = r * cap + s
                rows = pl.ds(pl.multiple_of(t % lanes_f * tile, tile), tile)
                chain[r, s + 1] = chain[r, table_s[r, s]] + nsend[t // lanes_f, rows, :].astype(F32)
            return carry

        lax.fori_loop(0, cap, link, 0)

    with scope("place"):

        def place(i, carry):
            def one(j, inner):
                for r in range(relations):
                    rows = pl.ds(pl.multiple_of(r * tn + i * tile, tile), tile)
                    cols = pl.ds(pl.multiple_of(j * tile, tile), tile)
                    a[rows, cols] = chain[r, table_s[relations + r, i * tile_cols_n + j]].astype(BF16)
                return inner

            return lax.fori_loop(0, tile_cols_n, one, carry)

        lax.fori_loop(0, tile_rows_n, place, 0)

    def forward(h, d):
        with scope(f"f{h}{d}" if isinstance(d, int) else f"f{h}"):
            slot = x_slot(h, x_from(d))
            remote(slot, slot, xs.at[0], xr.at[h, d - 1], sibling).wait_recv()
            remote(slot, slot, fs.at[0], fr.at[h, d], sibling).start()

    segments = max(tn // f, 1)
    seg = tn // segments

    def y_block(h, d):
        with scope(f"y{h}{d}"):
            slot = x_slot(h, me_c)
            remote(slot, slot, fs.at[0], fr.at[h, d], sibling).wait_recv()
            both = pl.ds(pl.multiple_of(lax.rem(z + nz - d, nz) * 2 * nd, 2 * nd), 2 * nd)
            for r in range(relations):
                part = jnp.dot(a[r * tn : (r + 1) * tn, both], xall[h, both, :], preferred_element_type=F32)
                for i in range(tile_rows_n):
                    for j in range(lanes_h):
                        b = part[i * tile : (i + 1) * tile, j * tile : (j + 1) * tile]
                        at = i * lanes_h + j
                        if d > 0:
                            b = b + chain[r, at]
                        if d < nz - 1:
                            chain[r, at] = b
                        else:
                            top = (i * tile // seg) * half + j * tile
                            side = (i * tile) % seg
                            w[r, top : top + tile, side : side + tile] = b.astype(BF16).T

    def c_copy(k):
        r, h = k % relations, k // relations
        return remote(pbuf.at[r, h], crecv.at[r, h], cs.at[0], cr.at[k], sibling)

    def held_rows(r, h, q):
        first = h * half + q * plane_rows
        block, off = first // tile, first % tile
        assert off + plane_rows <= tile
        return jnp.concatenate(
            [chain[r, held_at + block * lanes_f + j, off : off + plane_rows, :] for j in range(lanes_f)], axis=1
        )

    def terms(k):
        r, h = k % relations, k // relations
        with scope(f"terms{k}"):
            v = jnp.dot(w[r, 0:half, 0:seg], g[0:seg, :], preferred_element_type=F32)
            for s in range(1, segments):
                v = v + jnp.dot(
                    w[r, s * half : (s + 1) * half, 0:seg], g[s * seg : (s + 1) * seg, :], preferred_element_type=F32
                )
            for i in range(lanes_h):
                for j in range(lanes_f):
                    at = held_at + (h * lanes_h + i) * lanes_f + j
                    chain[r, at] = v[i * tile : (i + 1) * tile, j * tile : (j + 1) * tile]

            @pl.when(other)
            def _():
                for q in range(nr):
                    pbuf[r, h, q] = held_rows(r, h, q).astype(BF16)
                c_copy(k).start()

    def plane_scatter(k):
        r, h = k % relations, k // relations
        with scope(f"s1{k}"):
            c_copy(k).wait_recv()
            for q in range(nr):
                pbuf[r, h, q] = (held_rows(r, h, q) + crecv[r, h, q].astype(F32)).astype(BF16)
            begin([
                remote(pbuf.at[r, h, lax.rem(me_r + d, nr)], precv.at[k, d - 1], ps.at[0], pr.at[k], row_peer(d))
                for d in range(1, nr)
            ])

    def pa_copies(k):
        part = ag_ref.at[k % relations, k // relations, me_r]
        return [remote(part, part, aps.at[0], apr.at[k, d - 1], row_peer(d)) for d in range(1, nr)]

    def ca_copy(k, d):
        part = ag_ref.at[k % relations, k // relations, lax.rem(me_r + nr - d, nr)]
        return remote(part, part, acs.at[0], acr.at[0], sibling)

    def z_in(k, held):
        remote(zbuf.at[k, held], zrecv.at[k, last_hop], zs.at[0], zr.at[k, last_hop], z_at(inward)).start()

    def z_came(k, slot):
        remote(zrecv.at[k, slot], zrecv.at[k, slot], zs.at[0], zr.at[k, slot], sibling).wait_recv()

    def z_out(k):
        part = ag_ref.at[k % relations, k // relations, me_r]
        return remote(part, part, zos.at[0], zor.at[k], z_at(outward))

    def plane_sum(k):
        r, h = k % relations, k // relations
        remote(precv.at[k], precv.at[k], ps.at[0], pr.at[k], sibling).wait_recv()
        part = pbuf[r, h, me_r].astype(F32)
        for d in range(1, nr):
            part = part + precv[k, d - 1].astype(F32)
        zbuf[k, 0] = part.astype(BF16)

        @pl.when(jnp.logical_not(has_outer))
        def _():
            z_in(k, 0)

    def z_sum(k):
        @pl.when(has_outer)
        def _():
            z_came(k, 0)
            zbuf[k, 1] = (zbuf[k, 0].astype(F32) + zrecv[k, 0].astype(F32)).astype(BF16)
            z_in(k, 1)

    def plane_gather(k):
        @pl.when(inner)
        def _():
            z_came(k, 1)
            total = zbuf[k, passes].astype(F32) + zrecv[k, 1].astype(F32)
            ag_ref[k % relations, k // relations, me_r] = total.astype(BF16)

        @pl.when(jnp.logical_not(inner))
        def _():
            z_out(k).wait_recv()

        @pl.when(has_outer)
        def _():
            z_out(k).start()

        begin(pa_copies(k))
        ca_copy(k, 0).start()

    def core_gather(k):
        copies = pa_copies(k)
        for d in range(1, nr):
            copies[d - 1].wait_recv()
            ca_copy(k, d).start()

    def mix(k, carry):
        cols = pl.ds(pl.multiple_of(k * 2 * nd, 2 * nd), 2 * nd)
        both = jnp.dot(pt[...], a[:, cols], preferred_element_type=F32)
        nsend[k * 2] = both[:, :nd].astype(BF16)
        nsend[k * 2 + 1] = both[:, nd:].astype(BF16)
        return carry

    def n_core(part):
        span = slice(part * nz, (part + 1) * nz)
        return remote(nsend.at[span], nrecv.at[span], ns.at[0], nrs.at[part], sibling)

    def dn_send(k, p, slot, to):
        remote(nsend.at[k * 2 + p], ndst.at[slot, p], nzs.at[0], nzr.at[slot, p], z_at(to)).start()

    def dn_arrived(slot, p):
        came = ndst.at[slot, p]
        remote(came, came, nzs.at[0], nzr.at[slot, p], sibling).wait_recv()

    def dn_total(k, p):
        return nsend[k * 2 + p].astype(F32) + nrecv[k * 2 + p].astype(F32)

    def dn_first():
        for part in range(2):
            n_core(part).wait_recv()
        for j in range(nz - 1):
            up, down = nz - 1 - j, j
            for p in range(2):

                @pl.when(z == 0)
                def _():
                    nsend[up * 2 + p] = dn_total(up, p).astype(BF16)
                    dn_send(up, p, up + 1, 1)

                @pl.when(z == nz - 1)
                def _():
                    nsend[down * 2 + p] = dn_total(down, p).astype(BF16)
                    dn_send(down, p, down, nz - 2)

    def dn_pass(k, p, slot, to):
        dn_arrived(slot, p)
        nsend[k * 2 + p] = (dn_total(k, p) + ndst[slot, p].astype(F32)).astype(BF16)
        dn_send(k, p, slot, to)

    def dn_rest():
        for j in range(nz - 1):
            up, down = nz - 1 - j, j
            for p in range(2):

                @pl.when((z > 0) & (z < up))
                def _():
                    dn_pass(up, p, up + 1, z + 1)

                @pl.when((z > down) & (z < nz - 1))
                def _():
                    dn_pass(down, p, down, z - 1)

    own_dn = lambda: remote(nfin, dn_ref, nfs.at[0], nfr.at[0], sibling)

    def on_lead(*work):
        @pl.when(lead)
        def _():
            for w in work:
                w()

    def serve(*ks):
        on_lead(*[functools.partial(plane_scatter, k) for k in ks])

    y_block(0, 0)
    if nz > 1:
        forward(0, 1)
        y_block(0, 1)
    with scope("waitg"):
        load_w.wait()
        slots = gslot.at[0 : nr - 1]
        remote(slots, slots, gs.at[0], gr.at[0], sibling).wait_recv()
    with scope("premix"):
        for k in range(nr):
            g[:, k * width : (k + 1) * width] = gslot[k]
        for r in range(relations):
            pt[:, r * tn : (r + 1) * tn] = lax.dot_general(
                w[r], g[...], (((1,), (1,)), ((), ())), preferred_element_type=F32
            ).astype(BF16)

    def mix_step(k, carry):
        mix(k, carry)

        @pl.when(k < nz - 2)
        def _():
            forward(0, k + 2)

        @pl.when(lead & (k == nz // 2 - 1))
        def _():
            n_core(0).start()

        return carry

    with scope("mix"):
        lax.fori_loop(0, nz, mix_step, 0)
    on_lead(lambda: n_core(1).start())
    for d in range(2, nz):
        y_block(0, d)

    @pl.when(other)
    def _():
        with scope("dn_first"):
            dn_first()

    for k in range(relations):
        terms(k)
    for d in range(nz):
        if d > 0:
            forward(1, d)
            y_block(1, d - 1)
        if 0 < d <= relations:
            serve(d - 1)
    for d in range(nz, relations + 1):
        serve(d - 1)
    y_block(1, nz - 1)
    for k in range(relations, chunks):
        terms(k)

    stages = {1: plane_scatter, 2: plane_sum, 3: z_sum, 4: plane_gather, 5: core_gather}

    def reduce_all(hops):
        for stage, k in reduce_order(chunks, relations, hops):
            with scope(f"s{stage}_{k}"):
                stages[stage](k)

    @pl.when(lead & inner)
    def _():
        reduce_all(nz // 2)

    @pl.when(lead & jnp.logical_not(inner))
    def _():
        reduce_all(nz - 1)

    @pl.when(lead)
    def _():
        with scope("end"):
            own_dn().wait_recv()
            sent = nsend.at[0 : nz * 2]
            for ref, sem in ((sent, ns), (precv, ps), (zbuf.at[:, 0], zs), (precv, aps), (ag_ref, acs)):
                remote(ref, ref, sem.at[0], sem.at[0], sibling).wait_send()

            @pl.when(has_outer)
            def _():
                remote(zbuf.at[:, 0], zbuf.at[:, 0], zos.at[0], zos.at[0], sibling).wait_send()

    @pl.when(other)
    def _():
        with scope("dn_rest"):
            dn_rest()
        with scope("dn_fin"):
            for p in range(2):

                @pl.when(z > 0)
                def _():
                    dn_arrived(z + 1, p)

                @pl.when(z < nz - 1)
                def _():
                    dn_arrived(z, p)

                own = nsend[z * 2 + p].astype(F32) + nrecv[z * 2 + p].astype(F32)
                below = jnp.where(z > 0, ndst[z + 1, p].astype(F32), 0.0)
                above = jnp.where(z < nz - 1, ndst[z, p].astype(F32), 0.0)
                done = (own + below + above).T.astype(BF16)
                if p == 0:
                    dn_ref[...] = done
                else:
                    nfin[...] = done
            own_dn().start()
        with scope("oend"):
            remote(ag_ref, ag_ref, acs.at[0], acr.at[0], sibling).wait_recv()
            sent = nsend.at[0 : (nz - 1) * 2]
            for ref, sem in ((pbuf, cs), (sent, nzs), (nfin, nfs)):
                remote(ref, ref, sem.at[0], sem.at[0], sibling).wait_send()

    sent_x = xall.at[:, 0 : (nz - 1) * nd, :]
    sent_f = xall.at[:, 0 : nz * nd, :]
    for ref, sem in ((gslot.at[0 : nr - 1], gs), (sent_x, xs), (sent_f, fs)):
        remote(ref, ref, sem.at[0], sem.at[0], sibling).wait_send()


def widen_kernel(dn_ref, dw_ref, dn_out, dw_out, wide, out_sem):
    parts, rows = wide.shape[0], wide.shape[1]
    stores = [
        pltpu.make_async_copy(wide.at[k], dw_out.at[k * rows : (k + 1) * rows, :], out_sem.at[k])
        for k in range(parts)
    ]
    stores.append(pltpu.make_async_copy(dn_ref, dn_out, out_sem.at[parts]))
    stores[parts].start()
    for k in range(parts):
        wide[k] = dw_ref[k * rows : (k + 1) * rows, :].astype(F32)
        stores[k].start()
    for c in stores:
        c.wait()


def widen(d_nodes, gathered):
    total, f = gathered.shape
    parts = 6 if total % 96 == 0 else 1
    rows = total // parts
    hbm = pl.BlockSpec(memory_space=pltpu.HBM)
    vmem = pl.BlockSpec(memory_space=pltpu.VMEM)
    return pl.pallas_call(
        widen_kernel,
        in_specs=[vmem, vmem],
        out_specs=(hbm, hbm),
        out_shape=(
            jax.ShapeDtypeStruct(d_nodes.shape, BF16),
            jax.ShapeDtypeStruct(gathered.shape, F32),
        ),
        scratch_shapes=[
            pltpu.VMEM((parts, rows, f), F32),
            pltpu.SemaphoreType.DMA((parts + 1,)),
        ],
    )(
        pltpu.with_memory_space_constraint(d_nodes, pltpu.VMEM),
        pltpu.with_memory_space_constraint(gathered, pltpu.VMEM),
    )


def body(nr, nc, out_grad, node_in, weights, tile_vals, tile_rows, tile_cols, tile_count):
    relations, f = weights.shape[0], weights.shape[1]
    cap, tile = tile_vals.shape[3], tile_vals.shape[4]
    tn, width = out_grad.shape
    nd = node_in.shape[0]
    sn = nd * nc
    nz = nc // 2
    half = f // HALVES
    plane_rows = half // nr
    chunks = relations * HALVES
    assert nz % 2 == 0
    places = (tn // tile) * (sn // tile)
    spread = -(-max(places, cap) // 128) * 128
    blocks = max(cap + 1, (tn // tile) * (half // tile) + (f // tile) ** 2)
    slots = relations * cap * tile // f
    assert nd == tile and slots * f == relations * cap * tile
    dma = lambda *n: pltpu.SemaphoreType.DMA(n)
    hbm = pl.BlockSpec(memory_space=pltpu.HBM)
    vmem = pl.BlockSpec(memory_space=pltpu.VMEM)
    d_nodes, gathered = pl.pallas_call(
        functools.partial(main_kernel, nr, nc, relations, sn // tile),
        out_shape=(
            pltpu.VMEM((nd, f), BF16),
            pltpu.VMEM((relations, HALVES, nr, plane_rows, f), BF16),
        ),
        in_specs=[hbm] * 7,
        out_specs=(vmem, vmem),
        scratch_shapes=[
            pltpu.VMEM(tile_rows.shape, I32),
            pltpu.VMEM(tile_cols.shape, I32),
            pltpu.VMEM((1, relations), I32),
            pltpu.VMEM((-(-2 * relations // 8) * 8, spread), I32),
            pltpu.SMEM((-(-2 * relations // 8) * 8, spread), I32),
            pltpu.VMEM((relations, blocks, tile, tile), F32),
            pltpu.VMEM((nr, tn, width), BF16),
            pltpu.VMEM((tn, f), BF16),
            pltpu.VMEM(weights.shape, BF16),
            pltpu.VMEM((relations * tn, sn), BF16),
            pltpu.VMEM((HALVES, sn, half), BF16),
            pltpu.VMEM((f, relations * tn), BF16),
            pltpu.VMEM((max(nz * 2, slots), f, nd), BF16),
            pltpu.VMEM((nz * 2, f, nd), BF16),
            pltpu.VMEM((nz + 1, 2, f, nd), BF16),
            pltpu.VMEM((nd, f), BF16),
            pltpu.VMEM((relations, HALVES, nr, plane_rows, f), BF16),
            pltpu.VMEM((relations, HALVES, nr, plane_rows, f), BF16),
            pltpu.VMEM((chunks, nr - 1, plane_rows, f), BF16),
            pltpu.VMEM((chunks, 2, plane_rows, f), BF16),
            pltpu.VMEM((chunks, 2, plane_rows, f), BF16),
            dma(4), dma(1), dma(2 + HALVES),
            dma(1), dma(1),
            dma(1), dma(HALVES, nz - 1),
            dma(1), dma(HALVES, nz),
            dma(1), dma(2),
            dma(1), dma(nz + 1, 2),
            dma(1), dma(1),
            dma(1), dma(chunks),
            dma(1), dma(chunks),
            dma(1), dma(chunks, 2),
            dma(1), dma(chunks),
            dma(1), dma(chunks, nr - 1),
            dma(1), dma(1),
        ],
        compiler_params=pltpu.CompilerParams(
            collective_id=0, has_side_effects=True, vmem_limit_bytes=63000 * 1024
        ),
    )(
        tile_rows,
        tile_cols,
        tile_count.reshape(1, relations),
        tile_vals.reshape(slots, f, tile),
        out_grad,
        node_in,
        weights,
    )
    d_nodes, d_weights = widen(d_nodes, gathered.reshape(relations * f, f))
    return d_nodes, d_weights.reshape(relations, f, f)


def solution(mesh):
    return jax.shard_map(
        functools.partial(body, mesh.shape["row"], mesh.shape["col"]),
        mesh=mesh,
        in_specs=(
            P("col", "row"),
            P(("row", "col"), None),
            P(),
            P(None, "col", "row", None, None, None),
            P(None, "col", "row", None),
            P(None, "col", "row", None),
            P(None, "col", "row"),
        ),
        out_specs=(P(("row", "col"), None), P()),
        check_vma=False,
    )
```

time: 55.8 us -> 49.9 us (0.89)
  Pallas kernels: 55 us -> 49.1 us
    pallas_call x1, Pallas kernels: 53.2 us -> 47.3 us  [body(): pl.pallas_call(functools.partial(main_kernel, nr, nc, relations, sn // ti...]
where the time goes in v2:
time: 49.9 us; the launch traced here: 49.7 us
  Pallas kernels  49.1 us (98%)
  between operations  0.64 us (1%)
    pallas_call x1, Pallas kernels, body(): pl.pallas_call(functools.partial(main_kernel, nr, nc, relations, sn // ti...  47.3 us
    pallas_call x1, Pallas kernels, widen(): pl.pallas_call(widen_kernel, in_specs=[vmem, vmem], out_specs=(hbm, hbm),...  1.76 us

profile of v2, /device:TPU:0, one launch (start us, length us, event | category | flops | bytes accessed | tf_op | source)
XLA Modules:
  0.0 49.7 jit_solution(14958971188847070099)
XLA Ops:
  0.6 47.3 %shard_map.86 = (bf16[128,512]{1,0:T(8,128)(2,1)S(1)}, bf16[3,2,4,64,512]{4,3,2,1,0:T(8,128)(2,1)S(1)}) custom-call(s32[3,1,1,32]{3,2,1,0:T(1,128)} %rows_hbm.1, s32[3,1,1,32]{3,2,1,0:T(1,128)} %cols_hbm.1, s32[1,3]{1,0:T(1,128)} %bitcast.6, bf16[24,512,128]{2,1,0:T(8,128)(2,1)} %bitcast.5, bf16[512,128]{1,0:T(8,128)(2,1)} %grad_hbm.1, ...), custom_call_target="tpu_custom_call" | custom-call | tf_op jit(solution)/shard_map/pallas_call | solution.py:551
  47.9 1.8 %shard_map.87 = (bf16[128,512]{1,0:T(8,128)(2,1)}, f32[1536,512]{1,0:T(8,128)}) custom-call(bf16[128,512]{1,0:T(8,128)(2,1)S(1)} %get-tuple-element.6.dn_ref, bf16[1536,512]{1,0:T(8,128)(2,1)S(1)} %bitcast.4), custom_call_target="tpu_custom_call" | custom-call | tf_op jit(solution)/shard_map/pallas_call | solution.py:514

commit v3 on v2

--- a/solution.py
+++ b/solution.py
@@ -12,17 +12,22 @@
 BF16 = jnp.bfloat16
 I32 = jnp.int32
 HALVES = 2
+WIDE = 1
 scope = jax.named_scope
 
 
-def reduce_order(chunks, first, hops):
-    link, hop, late = 1.4, 2.6, 1.1
+def reduce_order(chunks, first, half_line, wide):
+    link, hop, late = 1.4, 3.6, 0.3
     events = []
     for k in range(chunks):
         t = link * k + (late if k >= first else 0.0)
         if k >= first:
-            events.append((1.0 + 0.1 * k, 1, k))
-        events += [(t, 2, k), (t + hop, 3, k), (t + hops * hop, 4, k), (t + hops * hop + 3.6, 5, k)]
+            events.append((0.5 + 0.1 * k, 1, k))
+        if k > 0:
+            events.append((t, 2, k))
+        met = t + half_line * hop + 0.4
+        out = 0.3 if k < wide else (half_line - 1) * 2.8
+        events += [(t + hop, 3, k), (met, 4, k), (met + out, 5, k), (met + 9.0, 6, k)]
     return [(stage, k) for _, stage, k in sorted(events)]
 
 
@@ -33,7 +38,7 @@
     rows_v, cols_v, count_v, table_v, table_s, chain, gslot, g, w, a, xall, pt,
     nsend, nrecv, ndst, nfin, pbuf, crecv, precv, zbuf, zrecv,
     small_sem, val_sem, load_sem, gs, gr, xs, xr, fs, fr, ns, nrs, nzs, nzr, nfs, nfr,
-    cs, cr, ps, pr, zs, zr, zos, zor, aps, apr, acs, acr,
+    cs, cr, ps, pr, zs, zr, aps, apr, acs, acr,
 ):
     nz = nc // 2
     cap, tile = rows_v.shape[3], chain.shape[2]
@@ -54,8 +59,16 @@
     lead = core == 1
     other = core == 0
 
+    def row_at(d):
+        at, bit = me_r, 1
+        while bit < nr:
+            if d & bit:
+                at = at + bit - 2 * bit * lax.rem(at // bit, 2)
+            bit *= 2
+        return at
+
     def row_peer(d):
-        return {"row": lax.rem(me_r + d, nr)}
+        return {"row": row_at(d)}
 
     def z_at(k):
         return {"col": k * 2 + core}
@@ -65,11 +78,11 @@
 
     left_side = z < nz // 2
     inward = jnp.where(left_side, z + 1, z - 1)
-    outward = jnp.where(left_side, z - 1, z + 1)
     has_outer = (z > 0) & (z < nz - 1)
     inner = (z == nz // 2 - 1) | (z == nz // 2)
-    last_hop = jnp.where(inner, 1, 0)
-    passes = jnp.where(has_outer, 1, 0)
+    side = jnp.where(left_side, 1, 2)
+    outward = jnp.where(left_side, z - 1, z + 1)
+    wide = min(WIDE, chunks)
 
     def remote(src, dst, send, recv, dev):
         return pltpu.make_async_remote_copy(
@@ -139,11 +152,15 @@
     with scope("sends"):
         mine = gslot.at[me_r]
         begin([remote(mine, mine, gs.at[0], gr.at[0], row_peer(d)) for d in range(1, nr)])
-        for h in range(HALVES):
+
+        def send_x(h):
             load_x[h].wait()
             own = x_slot(h, me_c)
+
             begin([remote(own, own, xs.at[0], xr.at[h, d - 1], z_peer(d)) for d in range(1, nz)])
             remote(own, own, fs.at[0], fr.at[h, 0], sibling).start()
+
+        send_x(0)
 
     with scope("chain"):
         load_table.wait()
@@ -234,14 +251,14 @@
                     pbuf[r, h, q] = held_rows(r, h, q).astype(BF16)
                 c_copy(k).start()
 
-    def plane_scatter(k):
-        r, h = k % relations, k // relations
-        with scope(f"s1{k}"):
-            c_copy(k).wait_recv()
+    def plane_scatter(r, h):
+        k = h * relations + r
+        with scope(f"s1_h{h}"):
+            remote(pbuf.at[r, h], crecv.at[r, h], cs.at[0], cr.at[k], sibling).wait_recv()
             for q in range(nr):
                 pbuf[r, h, q] = (held_rows(r, h, q) + crecv[r, h, q].astype(F32)).astype(BF16)
             begin([
-                remote(pbuf.at[r, h, lax.rem(me_r + d, nr)], precv.at[k, d - 1], ps.at[0], pr.at[k], row_peer(d))
+                remote(pbuf.at[r, h, row_at(d)], precv.at[k, d - 1], ps.at[0], pr.at[k], row_peer(d))
                 for d in range(1, nr)
             ])
 
@@ -250,18 +267,26 @@
         return [remote(part, part, aps.at[0], apr.at[k, d - 1], row_peer(d)) for d in range(1, nr)]
 
     def ca_copy(k, d):
-        part = ag_ref.at[k % relations, k // relations, lax.rem(me_r + nr - d, nr)]
+        part = ag_ref.at[k % relations, k // relations, row_at(d)]
         return remote(part, part, acs.at[0], acr.at[0], sibling)
 
-    def z_in(k, held):
-        remote(zbuf.at[k, held], zrecv.at[k, last_hop], zs.at[0], zr.at[k, last_hop], z_at(inward)).start()
+    def z_hand(k, held):
+        sent = zbuf.at[k, held]
+
+        @pl.when(inner)
+        def _():
+            if k < wide:
+                for d in range(1, nz):
+                    remote(sent, zrecv.at[k, side], zs.at[d - 1], zr.at[k, side], z_peer(d)).start()
+            else:
+                remote(sent, zrecv.at[k, side], zs.at[0], zr.at[k, side], z_at(inward)).start()
+
+        @pl.when(jnp.logical_not(inner))
+        def _():
+            remote(sent, zrecv.at[k, 0], zs.at[0], zr.at[k, 0], z_at(inward)).start()
 
     def z_came(k, slot):
         remote(zrecv.at[k, slot], zrecv.at[k, slot], zs.at[0], zr.at[k, slot], sibling).wait_recv()
-
-    def z_out(k):
-        part = ag_ref.at[k % relations, k // relations, me_r]
-        return remote(part, part, zos.at[0], zor.at[k], z_at(outward))
 
     def plane_sum(k):
         r, h = k % relations, k // relations
@@ -273,32 +298,45 @@
 
         @pl.when(jnp.logical_not(has_outer))
         def _():
-            z_in(k, 0)
+            z_hand(k, 0)
 
     def z_sum(k):
         @pl.when(has_outer)
         def _():
             z_came(k, 0)
             zbuf[k, 1] = (zbuf[k, 0].astype(F32) + zrecv[k, 0].astype(F32)).astype(BF16)
-            z_in(k, 1)
-
-    def plane_gather(k):
-        @pl.when(inner)
-        def _():
-            z_came(k, 1)
-            total = zbuf[k, passes].astype(F32) + zrecv[k, 1].astype(F32)
-            ag_ref[k % relations, k // relations, me_r] = total.astype(BF16)
-
-        @pl.when(jnp.logical_not(inner))
-        def _():
-            z_out(k).wait_recv()
-
-        @pl.when(has_outer)
-        def _():
-            z_out(k).start()
-
+            z_hand(k, 1)
+
+    def z_out(k):
+        part = ag_ref.at[k % relations, k // relations, me_r]
+        return remote(part, part, zs.at[1], zr.at[k, 1], z_at(outward))
+
+    def gather_on(k):
         begin(pa_copies(k))
         ca_copy(k, 0).start()
+
+    def inner_gather(k):
+        @pl.when(inner)
+        def _():
+            z_came(k, 3 - side)
+            own = zbuf[k, jnp.where(has_outer, 1, 0)].astype(F32)
+            ag_ref[k % relations, k // relations, me_r] = (own + zrecv[k, 3 - side].astype(F32)).astype(BF16)
+            if k >= wide:
+                pl.when(has_outer)(lambda: z_out(k).start())
+            gather_on(k)
+
+    def outer_gather(k):
+        @pl.when(jnp.logical_not(inner))
+        def _():
+            if k < wide:
+                z_came(k, 1)
+                z_came(k, 2)
+                both = zrecv[k, 1].astype(F32) + zrecv[k, 2].astype(F32)
+                ag_ref[k % relations, k // relations, me_r] = both.astype(BF16)
+            else:
+                z_out(k).wait_recv()
+                pl.when(has_outer)(lambda: z_out(k).start())
+            gather_on(k)
 
     def core_gather(k):
         copies = pa_copies(k)
@@ -313,9 +351,9 @@
         nsend[k * 2 + 1] = both[:, nd:].astype(BF16)
         return carry
 
-    def n_core(part):
-        span = slice(part * nz, (part + 1) * nz)
-        return remote(nsend.at[span], nrecv.at[span], ns.at[0], nrs.at[part], sibling)
+    def n_core(k):
+        span = pl.ds(2 * k, 2)
+        return remote(nsend.at[span], nrecv.at[span], ns.at[0], nrs.at[k], sibling)
 
     def dn_send(k, p, slot, to):
         remote(nsend.at[k * 2 + p], ndst.at[slot, p], nzs.at[0], nzr.at[slot, p], z_at(to)).start()
@@ -328,8 +366,8 @@
         return nsend[k * 2 + p].astype(F32) + nrecv[k * 2 + p].astype(F32)
 
     def dn_first():
-        for part in range(2):
-            n_core(part).wait_recv()
+        for k in range(nz):
+            n_core(k).wait_recv()
         for j in range(nz - 1):
             up, down = nz - 1 - j, j
             for p in range(2):
@@ -349,34 +387,50 @@
         nsend[k * 2 + p] = (dn_total(k, p) + ndst[slot, p].astype(F32)).astype(BF16)
         dn_send(k, p, slot, to)
 
+    def dn_up():
+        def step(m, carry):
+            up, p = nz - 1 - m // 2, m % 2
+
+            @pl.when((z > 0) & (z < up))
+            def _():
+                dn_pass(up, p, up + 1, z + 1)
+
+            return carry
+
+        lax.fori_loop(0, 2 * (nz - 1), step, 0)
+
+    def dn_down():
+        def step(m, carry):
+            down, p = m // 2, m % 2
+
+            @pl.when((z > down) & (z < nz - 1))
+            def _():
+                dn_pass(down, p, down, z - 1)
+
+            return carry
+
+        lax.fori_loop(0, 2 * (nz - 1), step, 0)
+
     def dn_rest():
-        for j in range(nz - 1):
-            up, down = nz - 1 - j, j
-            for p in range(2):
-
-                @pl.when((z > 0) & (z < up))
-                def _():
-                    dn_pass(up, p, up + 1, z + 1)
-
-                @pl.when((z > down) & (z < nz - 1))
-                def _():
-                    dn_pass(down, p, down, z - 1)
+        @pl.when(left_side)
+        def _():
+            dn_up()
+            dn_down()
+
+        @pl.when(jnp.logical_not(left_side))
+        def _():
+            dn_down()
+            dn_up()
 
     own_dn = lambda: remote(nfin, dn_ref, nfs.at[0], nfr.at[0], sibling)
-
-    def on_lead(*work):
-        @pl.when(lead)
-        def _():
-            for w in work:
-                w()
-
-    def serve(*ks):
-        on_lead(*[functools.partial(plane_scatter, k) for k in ks])
 
     y_block(0, 0)
     if nz > 1:
         forward(0, 1)
         y_block(0, 1)
+    for h in range(1, HALVES):
+        with scope("sends1"):
+            send_x(h)
     with scope("waitg"):
         load_w.wait()
         slots = gslot.at[0 : nr - 1]
@@ -389,70 +443,93 @@
                 w[r], g[...], (((1,), (1,)), ((), ())), preferred_element_type=F32
             ).astype(BF16)
 
-    def mix_step(k, carry):
+    def lead_mix(k, carry):
         mix(k, carry)
-
-        @pl.when(k < nz - 2)
-        def _():
-            forward(0, k + 2)
-
-        @pl.when(lead & (k == nz // 2 - 1))
-        def _():
-            n_core(0).start()
-
+        n_core(k).start()
         return carry
 
-    with scope("mix"):
-        lax.fori_loop(0, nz, mix_step, 0)
-    on_lead(lambda: n_core(1).start())
+    def other_mix(k, carry):
+        mix(k, carry)
+
+        @pl.when(k > 0)
+        def _():
+            forward(1, k)
+
+        return carry
+
+    for d in range(2, nz):
+        forward(0, d)
+
+    @pl.when(lead)
+    def _():
+        with scope("mix"):
+            lax.fori_loop(0, nz, lead_mix, 0)
+
     for d in range(2, nz):
         y_block(0, d)
+    for k in range(relations):
+        terms(k)
+
+        @pl.when(lead)
+        def _():
+            plane_scatter(k, 0)
+
+    @pl.when(lead)
+    def _():
+        for d in range(1, nz):
+            forward(1, d)
 
     @pl.when(other)
     def _():
+        with scope("mix"):
+            lax.fori_loop(0, nz, other_mix, 0)
         with scope("dn_first"):
             dn_first()
 
-    for k in range(relations):
-        terms(k)
     for d in range(nz):
-        if d > 0:
-            forward(1, d)
-            y_block(1, d - 1)
-        if 0 < d <= relations:
-            serve(d - 1)
-    for d in range(nz, relations + 1):
-        serve(d - 1)
-    y_block(1, nz - 1)
+        y_block(1, d)
+
+    @pl.when(lead)
+    def _():
+        with scope("s2_0"):
+            plane_sum(0)
+
     for k in range(relations, chunks):
         terms(k)
 
-    stages = {1: plane_scatter, 2: plane_sum, 3: z_sum, 4: plane_gather, 5: core_gather}
-
-    def reduce_all(hops):
-        for stage, k in reduce_order(chunks, relations, hops):
+    stages = {
+        1: lambda k: plane_scatter(k - relations, 1),
+        2: plane_sum,
+        3: z_sum,
+        4: inner_gather,
+        5: outer_gather,
+        6: core_gather,
+    }
+
+    @pl.when(lead)
+    def _():
+        for stage, k in reduce_order(chunks, relations, nz // 2, wide):
             with scope(f"s{stage}_{k}"):
                 stages[stage](k)
-
-    @pl.when(lead & inner)
-    def _():
-        reduce_all(nz // 2)
-
-    @pl.when(lead & jnp.logical_not(inner))
-    def _():
-        reduce_all(nz - 1)
-
-    @pl.when(lead)
-    def _():
         with scope("end"):
             own_dn().wait_recv()
             sent = nsend.at[0 : nz * 2]
             for ref, sem in ((sent, ns), (precv, ps), (zbuf.at[:, 0], zs), (precv, aps), (ag_ref, acs)):
                 remote(ref, ref, sem.at[0], sem.at[0], sibling).wait_send()
 
+            def z_left(count, at):
+                if count > 0:
+                    ref = zbuf.at[0:count, 0]
+                    remote(ref, ref, zs.at[at], zs.at[at], sibling).wait_send()
+
             @pl.when(has_outer)
             def _():
-                remote(zbuf.at[:, 0], zbuf.at[:, 0], zos.at[0], zos.at[0], sibling).wait_send()
+                z_left(chunks - wide, 1)
+
+            @pl.when(inner)
+            def _():
+                for d in range(2, nz):
+                    z_left(wide, d - 1)
 
     @pl.when(other)
     def _():
@@ -539,7 +616,7 @@
     half = f // HALVES
     plane_rows = half // nr
     chunks = relations * HALVES
-    assert nz % 2 == 0
+    assert nz % 2 == 0 and nr & (nr - 1) == 0
     places = (tn // tile) * (sn // tile)
     spread = -(-max(places, cap) // 128) * 128
     blocks = max(cap + 1, (tn // tile) * (half // tile) + (f // tile) ** 2)
@@ -577,18 +654,17 @@
             pltpu.VMEM((relations, HALVES, nr, plane_rows, f), BF16),
             pltpu.VMEM((chunks, nr - 1, plane_rows, f), BF16),
             pltpu.VMEM((chunks, 2, plane_rows, f), BF16),
-            pltpu.VMEM((chunks, 2, plane_rows, f), BF16),
+            pltpu.VMEM((chunks, 3, plane_rows, f), BF16),
             dma(4), dma(1), dma(2 + HALVES),
             dma(1), dma(1),
             dma(1), dma(HALVES, nz - 1),
             dma(1), dma(HALVES, nz),
-            dma(1), dma(2),
+            dma(1), dma(nz),
             dma(1), dma(nz + 1, 2),
             dma(1), dma(1),
             dma(1), dma(chunks),
             dma(1), dma(chunks),
-            dma(1), dma(chunks, 2),
-            dma(1), dma(chunks),
+            dma(max(nz - 1, 2)), dma(chunks, 3),
             dma(1), dma(chunks, nr - 1),
             dma(1), dma(1),
         ],

time: 49.9 us -> 47.5 us (0.952)
  Pallas kernels: 49.1 us -> 46.7 us
    pallas_call x1, Pallas kernels: 47.3 us -> 44.9 us  [body(): pl.pallas_call(functools.partial(main_kernel, nr, nc, relations, sn // ti...]
where the time goes in v3:
time: 47.5 us; the launch traced here: 47.3 us
  Pallas kernels  46.7 us (98%)
  between operations  0.64 us (1%)
    pallas_call x1, Pallas kernels, body(): pl.pallas_call(functools.partial(main_kernel, nr, nc, relations, sn // ti...  44.9 us
    pallas_call x1, Pallas kernels, widen(): pl.pallas_call(widen_kernel, in_specs=[vmem, vmem], out_specs=(hbm, hbm),...  1.76 us

profile of v3, /device:TPU:0, one launch (start us, length us, event | category | flops | bytes accessed | tf_op | source)
XLA Modules:
  0.0 47.3 jit_solution(5595284620981191584)
XLA Ops:
  0.6 44.9 %shard_map.86 = (bf16[128,512]{1,0:T(8,128)(2,1)S(1)}, bf16[3,2,4,64,512]{4,3,2,1,0:T(8,128)(2,1)S(1)}) custom-call(s32[3,1,1,32]{3,2,1,0:T(1,128)} %rows_hbm.1, s32[3,1,1,32]{3,2,1,0:T(1,128)} %cols_hbm.1, s32[1,3]{1,0:T(1,128)} %bitcast.6, bf16[24,512,128]{2,1,0:T(8,128)(2,1)} %bitcast.5, bf16[512,128]{1,0:T(8,128)(2,1)} %grad_hbm.1, ...), custom_call_target="tpu_custom_call" | custom-call | tf_op jit(solution)/shard_map/pallas_call | solution.py:628
  45.6 1.8 %shard_map.87 = (bf16[128,512]{1,0:T(8,128)(2,1)}, f32[1536,512]{1,0:T(8,128)}) custom-call(bf16[128,512]{1,0:T(8,128)(2,1)S(1)} %get-tuple-element.6.dn_ref, bf16[1536,512]{1,0:T(8,128)(2,1)S(1)} %bitcast.4), custom_call_target="tpu_custom_call" | custom-call | tf_op jit(solution)/shard_map/pallas_call | solution.py:591

commit v4 on v3

--- a/solution.py
+++ b/solution.py
@@ -365,22 +365,20 @@
     def dn_total(k, p):
         return nsend[k * 2 + p].astype(F32) + nrecv[k * 2 + p].astype(F32)
 
-    def dn_first():
-        for k in range(nz):
-            n_core(k).wait_recv()
-        for j in range(nz - 1):
-            up, down = nz - 1 - j, j
-            for p in range(2):
-
-                @pl.when(z == 0)
-                def _():
-                    nsend[up * 2 + p] = dn_total(up, p).astype(BF16)
-                    dn_send(up, p, up + 1, 1)
-
-                @pl.when(z == nz - 1)
-                def _():
-                    nsend[down * 2 + p] = dn_total(down, p).astype(BF16)
-                    dn_send(down, p, down, nz - 2)
+    at_end = (z == 0) | (z == nz - 1)
+
+    def dn_first(k):
+        n_core(k).wait_recv()
+        for p in range(2):
+            nsend[k * 2 + p] = dn_total(k, p).astype(BF16)
+
+            @pl.when(z == 0)
+            def _():
+                dn_send(k, p, k + 1, 1)
+
+            @pl.when(z > 0)
+            def _():
+                dn_send(k, p, k, nz - 2)
 
     def dn_pass(k, p, slot, to):
         dn_arrived(slot, p)
@@ -443,17 +441,26 @@
                 w[r], g[...], (((1,), (1,)), ((), ())), preferred_element_type=F32
             ).astype(BF16)
 
-    def lead_mix(k, carry):
+    def far_first(i):
+        return jnp.where(left_side, nz - 1 - i, i)
+
+    def lead_mix(i, carry):
+        k = far_first(i)
         mix(k, carry)
         n_core(k).start()
         return carry
 
-    def other_mix(k, carry):
+    def other_mix(i, carry):
+        k = far_first(i)
         mix(k, carry)
 
-        @pl.when(k > 0)
-        def _():
-            forward(1, k)
+        @pl.when(at_end & (k != z))
+        def _():
+            dn_first(k)
+
+        @pl.when(i > 0)
+        def _():
+            forward(1, i)
 
         return carry
 
@@ -483,8 +490,6 @@
     def _():
         with scope("mix"):
             lax.fori_loop(0, nz, other_mix, 0)
-        with scope("dn_first"):
-            dn_first()
 
     for d in range(nz):
         y_block(1, d)
@@ -533,6 +538,14 @@
 
     @pl.when(other)
     def _():
+        def mixed(k, carry):
+            @pl.when(jnp.logical_not(at_end & (k != z)))
+            def _():
+                n_core(k).wait_recv()
+
+            return carry
+
+        lax.fori_loop(0, nz, mixed, 0)
         with scope("dn_rest"):
             dn_rest()
         with scope("dn_fin"):

time: 47.5 us -> 46.5 us (0.979)
  Pallas kernels: 46.7 us -> 45.7 us
    pallas_call x1, Pallas kernels: 44.9 us -> 43.9 us  [body(): pl.pallas_call(functools.partial(main_kernel, nr, nc, relations, sn // ti...]
where the time goes in v4:
time: 46.5 us; the launch traced here: 46.3 us
  Pallas kernels  45.7 us (98%)
  between operations  0.64 us (1%)
    pallas_call x1, Pallas kernels, body(): pl.pallas_call(functools.partial(main_kernel, nr, nc, relations, sn // ti...  43.9 us
    pallas_call x1, Pallas kernels, widen(): pl.pallas_call(widen_kernel, in_specs=[vmem, vmem], out_specs=(hbm, hbm),...  1.76 us

profile of v4, /device:TPU:0, one launch (start us, length us, event | category | flops | bytes accessed | tf_op | source)
XLA Modules:
  0.0 46.3 jit_solution(13267965433609680167)
XLA Ops:
  0.6 43.9 %shard_map.86 = (bf16[128,512]{1,0:T(8,128)(2,1)S(1)}, bf16[3,2,4,64,512]{4,3,2,1,0:T(8,128)(2,1)S(1)}) custom-call(s32[3,1,1,32]{3,2,1,0:T(1,128)} %rows_hbm.1, s32[3,1,1,32]{3,2,1,0:T(1,128)} %cols_hbm.1, s32[1,3]{1,0:T(1,128)} %bitcast.6, bf16[24,512,128]{2,1,0:T(8,128)(2,1)} %bitcast.5, bf16[512,128]{1,0:T(8,128)(2,1)} %grad_hbm.1, ...), custom_call_target="tpu_custom_call" | custom-call | tf_op jit(solution)/shard_map/pallas_call | solution.py:641
  44.6 1.8 %shard_map.87 = (bf16[128,512]{1,0:T(8,128)(2,1)}, f32[1536,512]{1,0:T(8,128)}) custom-call(bf16[128,512]{1,0:T(8,128)(2,1)S(1)} %get-tuple-element.6.dn_ref, bf16[1536,512]{1,0:T(8,128)(2,1)S(1)} %bitcast.4), custom_call_target="tpu_custom_call" | custom-call | tf_op jit(solution)/shard_map/pallas_call | solution.py:604

commit v5 on v4

--- a/solution.py
+++ b/solution.py
@@ -259,7 +259,7 @@
                 pbuf[r, h, q] = (held_rows(r, h, q) + crecv[r, h, q].astype(F32)).astype(BF16)
             begin([
                 remote(pbuf.at[r, h, row_at(d)], precv.at[k, d - 1], ps.at[0], pr.at[k], row_peer(d))
-                for d in range(1, nr)
+                for d in range(nr - 1, 0, -1)
             ])
 
     def pa_copies(k):
@@ -312,7 +312,7 @@
         return remote(part, part, zs.at[1], zr.at[k, 1], z_at(outward))
 
     def gather_on(k):
-        begin(pa_copies(k))
+        begin(pa_copies(k)[::-1])
         ca_copy(k, 0).start()
 
     def inner_gather(k):

time: 46.5 us -> 45.8 us (0.985)
  Pallas kernels: 45.7 us -> 45 us
    pallas_call x1, Pallas kernels: 43.9 us -> 43.2 us  [body(): pl.pallas_call(functools.partial(main_kernel, nr, nc, relations, sn // ti...]
where the time goes in v5:
time: 45.8 us; the launch traced here: 45.6 us
  Pallas kernels  45 us (98%)
  between operations  0.64 us (1%)
    pallas_call x1, Pallas kernels, body(): pl.pallas_call(functools.partial(main_kernel, nr, nc, relations, sn // ti...  43.2 us
    pallas_call x1, Pallas kernels, widen(): pl.pallas_call(widen_kernel, in_specs=[vmem, vmem], out_specs=(hbm, hbm),...  1.76 us

profile of v5, /device:TPU:0, one launch (start us, length us, event | category | flops | bytes accessed | tf_op | source)
XLA Modules:
  0.0 45.6 jit_solution(1631370950819459720)
XLA Ops:
  0.6 43.2 %shard_map.86 = (bf16[128,512]{1,0:T(8,128)(2,1)S(1)}, bf16[3,2,4,64,512]{4,3,2,1,0:T(8,128)(2,1)S(1)}) custom-call(s32[3,1,1,32]{3,2,1,0:T(1,128)} %rows_hbm.1, s32[3,1,1,32]{3,2,1,0:T(1,128)} %cols_hbm.1, s32[1,3]{1,0:T(1,128)} %bitcast.6, bf16[24,512,128]{2,1,0:T(8,128)(2,1)} %bitcast.5, bf16[512,128]{1,0:T(8,128)(2,1)} %grad_hbm.1, ...), custom_call_target="tpu_custom_call" | custom-call | tf_op jit(solution)/shard_map/pallas_call | solution.py:641
  43.9 1.8 %shard_map.87 = (bf16[128,512]{1,0:T(8,128)(2,1)}, f32[1536,512]{1,0:T(8,128)}) custom-call(bf16[128,512]{1,0:T(8,128)(2,1)S(1)} %get-tuple-element.6.dn_ref, bf16[1536,512]{1,0:T(8,128)(2,1)S(1)} %bitcast.4), custom_call_target="tpu_custom_call" | custom-call | tf_op jit(solution)/shard_map/pallas_call | solution.py:604

commit v6 on v5

--- a/solution.py
+++ b/solution.py
@@ -264,7 +264,8 @@
 
     def pa_copies(k):
         part = ag_ref.at[k % relations, k // relations, me_r]
-        return [remote(part, part, aps.at[0], apr.at[k, d - 1], row_peer(d)) for d in range(1, nr)]
+        at = lambda d: k if k < chunks - 1 else k + d - 1
+        return [remote(part, part, aps.at[0], apr.at[at(d)], row_peer(d)) for d in range(1, nr)]
 
     def ca_copy(k, d):
         part = ag_ref.at[k % relations, k // relations, row_at(d)]
@@ -339,6 +340,10 @@
             gather_on(k)
 
     def core_gather(k):
+        if k < chunks - 1:
+            remote(precv.at[k], precv.at[k], aps.at[0], apr.at[k], sibling).wait_recv()
+            begin([ca_copy(k, d) for d in range(1, nr)])
+            return
         copies = pa_copies(k)
         for d in range(1, nr):
             copies[d - 1].wait_recv()
@@ -597,7 +602,7 @@
 
 def widen(d_nodes, gathered):
     total, f = gathered.shape
-    parts = 6 if total % 96 == 0 else 1
+    parts = 12 if total % 192 == 0 else 1
     rows = total // parts
     hbm = pl.BlockSpec(memory_space=pltpu.HBM)
     vmem = pl.BlockSpec(memory_space=pltpu.VMEM)
@@ -678,7 +683,7 @@
             dma(1), dma(chunks),
             dma(1), dma(chunks),
             dma(max(nz - 1, 2)), dma(chunks, 3),
-            dma(1), dma(chunks, nr - 1),
+            dma(1), dma(chunks - 1 + nr - 1),
             dma(1), dma(1),
         ],
         compiler_params=pltpu.CompilerParams(

time: 45.8 us -> 45.7 us (level)
  no operation moved by 1% of the time
where the time goes in v6:
time: 45.7 us; the launch traced here: 45.6 us
  Pallas kernels  44.9 us (98%)
  between operations  0.64 us (1%)
    pallas_call x1, Pallas kernels, body(): pl.pallas_call(functools.partial(main_kernel, nr, nc, relations, sn // ti...  43.1 us
    pallas_call x1, Pallas kernels, widen(): pl.pallas_call(widen_kernel, in_specs=[vmem, vmem], out_specs=(hbm, hbm),...  1.81 us

profile of v6, /device:TPU:0, one launch (start us, length us, event | category | flops | bytes accessed | tf_op | source)
XLA Modules:
  0.0 45.6 jit_solution(6872460604087134772)
XLA Ops:
  0.6 43.1 %shard_map.86 = (bf16[128,512]{1,0:T(8,128)(2,1)S(1)}, bf16[3,2,4,64,512]{4,3,2,1,0:T(8,128)(2,1)S(1)}) custom-call(s32[3,1,1,32]{3,2,1,0:T(1,128)} %rows_hbm.1, s32[3,1,1,32]{3,2,1,0:T(1,128)} %cols_hbm.1, s32[1,3]{1,0:T(1,128)} %bitcast.6, bf16[24,512,128]{2,1,0:T(8,128)(2,1)} %bitcast.5, bf16[512,128]{1,0:T(8,128)(2,1)} %grad_hbm.1, ...), custom_call_target="tpu_custom_call" | custom-call | tf_op jit(solution)/shard_map/pallas_call | solution.py:646
  43.8 1.8 %shard_map.87 = (bf16[128,512]{1,0:T(8,128)(2,1)}, f32[1536,512]{1,0:T(8,128)}) custom-call(bf16[128,512]{1,0:T(8,128)(2,1)S(1)} %get-tuple-element.6.dn_ref, bf16[1536,512]{1,0:T(8,128)(2,1)S(1)} %bitcast.4), custom_call_target="tpu_custom_call" | custom-call | tf_op jit(solution)/shard_map/pallas_call | solution.py:609
